TPU v7x, 32 devices: a whole 2x2x4 slice. The times are simulated.
32 devices in a mesh: kx: 4 (over z), ky: 4 (over y, x), kz: 2 (over core).
Axes of the slice: x: 2, y: 2, z: 4, core: 2. Of those that a mesh axis runs over, the one named last changes fastest.
Arguments:
- u_start: float32 [4, 4, 8, 2, 128, 128], P('kx', 'ky', 'kz'), may hold values from -1 to 1, as said below
- intersections: float32 [4, 4, 8, 12, 2, 128, 128], P('kx', 'ky', 'kz'), may hold values from -1.2 to 1.2, as said below
Outputs:
- u_final: float32 [4, 4, 8, 2, 128, 128], P('kx', 'ky', 'kz')
- centres: float32 [3, 3, 128], replicated
- spreads: float32 [3, 128], replicated
Inputs may be any that keep to these rules, and one draw needn't show every extreme that they name: `u_start`: each U(k) is unitary up to float32 rounding and close to the identity: every diagonal entry of U(k) has magnitude 0.7 or more. `intersections`: every diagonal entry of every M(k,b) has magnitude 0.45 or more and a phase within 1.9 of zero.
All inputs are finite; a program needn't handle non-finite values.
Results may differ from a plain program's by a relative error of at most 0.0003.
Values sent between devices are 32-bit elements; how exact they have to be, the bound alone decides.
A program may use at most 128 MiB of HBM per device.

v0:
```python
import jax
import jax.numpy as jnp
from jax import lax
from jax.sharding import PartitionSpec as P

ITERS = 3
OFFSETS = (
    (1, 1, 0),
    (1, -1, 0),
    (-1, 1, 0),
    (-1, -1, 0),
    (1, 0, 1),
    (1, 0, -1),
    (-1, 0, 1),
    (-1, 0, -1),
    (0, 1, 1),
    (0, 1, -1),
    (0, -1, 1),
    (0, -1, -1),
)
WEIGHT = 0.125
STEP_SIZE = 0.35
PRECISE = lax.Precision.HIGHEST


def extended(cells, sides, width):
    for axis, dim in sides:
        count = lax.axis_size(axis)
        head = lax.slice_in_dim(cells, 0, width, axis=dim)
        tail = lax.slice_in_dim(cells, cells.shape[dim] - width, cells.shape[dim], axis=dim)
        cells = jnp.concatenate(
            [
                lax.ppermute(tail, axis, [(i, (i + 1) % count) for i in range(count)]),
                cells,
                lax.ppermute(head, axis, [((i + 1) % count, i) for i in range(count)]),
            ],
            axis=dim,
        )
    return cells


def matmul(left, right):
    return jnp.einsum("...ij,...jk->...ik", left, right, precision=PRECISE)


def adjoint_product(left, right):
    return jnp.einsum("...ji,...jk->...ik", left, right, precision=PRECISE)


def complex_product(left_real, left_imag, right_real, right_imag):
    return (
        matmul(left_real, right_real) - matmul(left_imag, right_imag),
        matmul(left_real, right_imag) + matmul(left_imag, right_real),
    )


def gather_neighbours(unitary):
    extent_x = unitary.shape[0]
    extent_y = unitary.shape[1]
    extent_z = unitary.shape[2]
    padded = extended(unitary, (("kx", 0), ("ky", 1), ("kz", 2)), 1)
    pieces = []
    for offset in OFFSETS:
        pieces.append(
            padded[
                1 + offset[0] : 1 + offset[0] + extent_x,
                1 + offset[1] : 1 + offset[1] + extent_y,
                1 + offset[2] : 1 + offset[2] + extent_z,
            ]
        )
    return jnp.stack(pieces, axis=3)


def body(u_start, intersections):
    count_x = u_start.shape[0]
    count_y = u_start.shape[1]
    count_z = u_start.shape[2]
    width = u_start.shape[-1]
    total_points = (
        count_x
        * count_y
        * count_z
        * lax.axis_size("kx")
        * lax.axis_size("ky")
        * lax.axis_size("kz")
    )
    offset_table = jnp.array(OFFSETS, jnp.float32)
    identity = jnp.eye(width, dtype=jnp.float32)
    intersection_real = intersections[:, :, :, :, 0]
    intersection_imag = intersections[:, :, :, :, 1]
    unitary = u_start
    centre_list = []
    spread_list = []
    for iteration in range(ITERS):
        local_real = unitary[:, :, :, None, 0]
        local_imag = unitary[:, :, :, None, 1]
        left_real = adjoint_product(local_real, intersection_real) + adjoint_product(
            local_imag, intersection_imag
        )
        left_imag = adjoint_product(local_real, intersection_imag) - adjoint_product(
            local_imag, intersection_real
        )
        nearby = gather_neighbours(unitary)
        turned_real, turned_imag = complex_product(
            left_real, left_imag, nearby[:, :, :, :, 0], nearby[:, :, :, :, 1]
        )
        diagonal_real = jnp.diagonal(turned_real, axis1=-2, axis2=-1)
        diagonal_imag = jnp.diagonal(turned_imag, axis1=-2, axis2=-1)
        phases = jnp.arctan2(diagonal_imag, diagonal_real)
        magnitude = diagonal_real * diagonal_real + diagonal_imag * diagonal_imag
        first_sums = WEIGHT * jnp.einsum("xyzbn,bc->cn", phases, offset_table, precision=PRECISE)
        second_sums = WEIGHT * jnp.sum(1.0 - magnitude + phases * phases, axis=(0, 1, 2, 3))
        product_real = (
            turned_real * diagonal_real[..., None, :] + turned_imag * diagonal_imag[..., None, :]
        )
        product_imag = (
            turned_imag * diagonal_real[..., None, :] - turned_real * diagonal_imag[..., None, :]
        )
        first_total, second_total = lax.psum((first_sums, second_sums), ("kx", "ky", "kz"))
        centres = -first_total / total_points
        spreads = second_total / total_points - jnp.sum(centres * centres, axis=0)
        centre_list.append(centres)
        spread_list.append(spreads)
        shifted = phases + jnp.einsum("bc,cn->bn", offset_table, centres, precision=PRECISE)
        scaled = (shifted / magnitude)[..., None, :]
        summed_real = jnp.sum(product_real - product_imag * scaled, axis=3)
        summed_imag = jnp.sum(product_imag + product_real * scaled, axis=3)
        gradient_real = 2.0 * WEIGHT * (summed_real - jnp.swapaxes(summed_real, -1, -2))
        gradient_imag = 2.0 * WEIGHT * (summed_imag + jnp.swapaxes(summed_imag, -1, -2))
        change_real = STEP_SIZE * gradient_real
        change_imag = STEP_SIZE * gradient_imag
        inner_real = 0.5 * identity + change_real / 6.0
        inner_imag = change_imag / 6.0
        middle_real, middle_imag = complex_product(change_real, change_imag, inner_real, inner_imag)
        middle_real = identity + middle_real
        exponent_real, exponent_imag = complex_product(
            change_real, change_imag, middle_real, middle_imag
        )
        exponent_real = identity + exponent_real
        update_real, update_imag = complex_product(
            unitary[:, :, :, 0], unitary[:, :, :, 1], exponent_real, exponent_imag
        )
        unitary = jnp.stack([update_real, update_imag], axis=3)
    return (unitary, jnp.stack(centre_list), jnp.stack(spread_list))


def solution(mesh):
    in_specs = (P("kx", "ky", "kz", None, None, None), P("kx", "ky", "kz", None, None, None, None))
    out_specs = (P("kx", "ky", "kz", None, None, None), P(), P())
    return jax.shard_map(body, mesh=mesh, in_specs=in_specs, out_specs=out_specs, check_vma=False)
```

profile of v0, /device:TPU:0, one launch (start us, length us, event | category | flops | bytes accessed | tf_op | source)
XLA Modules:
  0.0 661.2 jit_solution(17291030890249032201)
XLA Ops:
  1.8 3.1 collective-permute-start
  4.9 2.1 collective-permute-start.1
  7.0 12.8 %collective-permute-done = f32[1,1,4,2,128,128]{5,4,2,3,1,0:T(8,128)S(1)} collective-permute-done((f32[1,1,4,2,128,128]{5,4,2,3,1,0:T(8,128)S(1)}, f32[1,1,4,2,128,128]{5,4,2,3,1,0:T(8,128)S(1)}, u32[]{:S(2)}, u32[]{:S(2)}) %collective-permute-start) | collective-permute-done | bytes 524320 | tf_op jit(solution)/shard_map/ppermute | solution.py:33
  20.9 8.7 %collective-permute-done.1 = f32[1,1,4,2,128,128]{5,4,2,3,1,0:T(8,128)S(1)} collective-permute-done((f32[1,1,4,2,128,128]{5,4,2,3,1,0:T(8,128)S(1)}, f32[1,1,4,2,128,128]{5,4,2,3,1,0:T(8,128)S(1)}, u32[]{:S(2)}, u32[]{:S(2)}) %collective-permute-start.1) | collective-permute-done | bytes 524320 | tf_op jit(solution)/shard_map/ppermute | solution.py:35
  32.5 7.0 %fusion.10 = f32[4,12,128,128]{3,2,1,0:T(8,128)S(1)} fusion(f32[1,1,4,12,2,128,128]{6,5,4,3,2,1,0:T(8,128)} %param.4, f32[1,1,4,2,128,128]{5,4,3,2,1,0:T(8,128)S(1)} %copy-done.1), kind=kOutput, calls=%fused_computation.22 | convolution fusion | flops 1207959552 | bytes 6553600 | tf_op jit(solution)/shard_map/...ji,...jk->...ik/dot_general | solution.py:47
  39.6 5.1 fusion.8
  44.7 5.2 fusion.94
  49.9 5.1 fusion.97
  55.0 12.8 %collective-permute-done.3 = f32[3,1,4,2,128,128]{5,4,2,3,1,0:T(8,128)S(1)} collective-permute-done((f32[3,1,4,2,128,128]{5,4,2,3,1,0:T(8,128)S(1)}, f32[3,1,4,2,128,128]{5,4,2,3,1,0:T(8,128)S(1)}, u32[]{:S(2)}, u32[]{:S(2)}) %collective-permute-start.3) | collective-permute-done | bytes 1572896 | tf_op jit(solution)/shard_map/ppermute | solution.py:33
  67.8 32.2 %collective-permute-done.2 = f32[3,1,4,2,128,128]{5,4,2,3,1,0:T(8,128)S(1)} collective-permute-done((f32[3,1,4,2,128,128]{5,4,2,3,1,0:T(8,128)S(1)}, f32[3,1,4,2,128,128]{5,4,2,3,1,0:T(8,128)S(1)}, u32[]{:S(2)}, u32[]{:S(2)}) %collective-permute-start.2) | collective-permute-done | bytes 1572896 | tf_op jit(solution)/shard_map/ppermute | solution.py:35
  101.1 2.1 collective-permute-done.4
  103.2 1.6 collective-permute-done.5
  105.2 5.7 fusion.40
  110.9 5.5 fusion.42
  116.3 6.0 fusion.71
  122.4 7.2 %fusion.68 = f32[4,12,128,128]{3,2,1,0:T(8,128)} fusion(f32[4,12,128,128]{3,2,1,0:T(8,128)S(1)} %fusion.42, f32[1,1,4,12,2,128,128]{6,5,3,2,4,1,0:T(8,128)S(1)} %fusion.152, f32[4,12,128,128]{3,2,1,0:T(8,128)S(1)} %fusion.94), kind=kOutput, calls=%fused_computation.92 | convolution fusion | flops 1208745984 | bytes 12582912 | tf_op jit(solution)/shard_map/...ij,...jk->...ik/dot_general | solution.py:43
  129.6 18.5 %copy.238 = f32[4,12,128,128]{1,0,3,2:T(4,128)} copy(f32[4,12,128,128]{3,2,1,0:T(8,128)} %fusion.68) | data formatting | bytes 6291456 | tf_op jit(solution)/shard_map/sub | solution.py:52
  148.1 1.9 gather_fusion
  151.4 16.8 %copy.243 = f32[4,12,128,128]{1,0,3,2:T(4,128)} copy(f32[4,12,128,128]{3,2,1,0:T(8,128)S(1)} %fusion.71) | data formatting | bytes 6291456 | tf_op jit(solution)/shard_map/add | solution.py:53
  168.2 1.9 gather_fusion.1
  173.0 39.8 %psum.42 = f32[3,128]{1,0:T(4,128)S(1)} all-reduce(f32[3,128]{1,0:T(4,128)} %fusion.122), channel_id=1, replica_groups=mesh['kx'=4,'ky'=4,'kz'=2] {'kx','ky','kz'}, use_global_device_ids=true, to_apply=%region_1.2 | all-reduce | flops 384 | bytes 3072 | tf_op jit(solution)/shard_map/psum | solution.py:119
  215.0 4.2 add_reduce_fusion.2
  226.5 1.6 collective-permute-start.7
  228.6 12.7 %collective-permute-done.7 = f32[1,1,4,2,128,128]{4,5,2,3,1,0:T(8,128)S(1)} collective-permute-done((f32[1,1,4,2,128,128]{4,5,2,3,1,0:T(8,128)S(1)}, f32[1,1,4,2,128,128]{4,5,2,3,1,0:T(8,128)S(1)}, u32[]{:S(2)}, u32[]{:S(2)}) %collective-permute-start.7) | collective-permute-done | bytes 524320 | tf_op jit(solution)/shard_map/ppermute | solution.py:35
  241.3 9.3 %collective-permute-done.6 = f32[1,1,4,2,128,128]{4,5,2,3,1,0:T(8,128)S(1)} collective-permute-done((f32[1,1,4,2,128,128]{4,5,2,3,1,0:T(8,128)S(1)}, f32[1,1,4,2,128,128]{4,5,2,3,1,0:T(8,128)S(1)}, u32[]{:S(2)}, u32[]{:S(2)}) %collective-permute-start.6) | collective-permute-done | bytes 524320 | tf_op jit(solution)/shard_map/ppermute | solution.py:33
  250.8 2.3 collective-permute-start.9
  254.0 3.0 fusion.6
  257.0 3.0 fusion.4
  260.0 3.0 fusion.100
  263.1 26.0 %collective-permute-done.9 = f32[3,1,4,2,128,128]{4,5,2,3,1,0:T(8,128)S(1)} collective-permute-done((f32[3,1,4,2,128,128]{4,5,2,3,1,0:T(8,128)S(1)}, f32[3,1,4,2,128,128]{4,5,2,3,1,0:T(8,128)S(1)}, u32[]{:S(2)}, u32[]{:S(2)}) %collective-permute-start.9) | collective-permute-done | bytes 1572896 | tf_op jit(solution)/shard_map/ppermute | solution.py:33
  289.1 31.8 %collective-permute-done.8 = f32[3,1,4,2,128,128]{4,5,2,3,1,0:T(8,128)S(1)} collective-permute-done((f32[3,1,4,2,128,128]{4,5,2,3,1,0:T(8,128)S(1)}, f32[3,1,4,2,128,128]{4,5,2,3,1,0:T(8,128)S(1)}, u32[]{:S(2)}, u32[]{:S(2)}) %collective-permute-start.8) | collective-permute-done | bytes 1572896 | tf_op jit(solution)/shard_map/ppermute | solution.py:35
  321.6 3.0 fusion.103
  327.2 6.8 %fusion.34 = f32[4,12,128,128]{3,2,1,0:T(8,128)S(1)} fusion(f32[4,128,12,128]{3,1,2,0:T(8,128)S(1)} %fusion.103, f32[4,12,128,128]{2,3,0,1:T(8,128)S(1)} %get-tuple-element.33), kind=kOutput, calls=%fused_computation.46 | convolution fusion | flops 1207959552 | bytes 9437184 | tf_op jit(solution)/shard_map/...ij,...jk->...ik/dot_general | solution.py:43
  334.0 6.7 %fusion.32 = f32[4,12,128,128]{3,2,1,0:T(8,128)S(1)} fusion(f32[4,128,12,128]{3,1,2,0:T(8,128)S(1)} %fusion.103, f32[4,12,128,128]{2,3,0,1:T(8,128)S(1)} %get-tuple-element.34), kind=kOutput, calls=%fused_computation.44 | convolution fusion | flops 1207959552 | bytes 9437184 | tf_op jit(solution)/shard_map/...ij,...jk->...ik/dot_general | solution.py:43
  340.7 8.6 %fusion.74 = f32[4,12,128,128]{3,2,1,0:T(8,128)} fusion(f32[4,12,128,128]{3,2,1,0:T(8,128)S(1)} %fusion.34, f32[4,12,128,128]{2,3,0,1:T(8,128)S(1)} %get-tuple-element.34, f32[4,128,12,128]{3,1,2,0:T(8,128)S(1)} %fusion.100), kind=kOutput, calls=%fused_computation.94 | convolution fusion | flops 1208745984 | bytes 12582912 | tf_op jit(solution)/shard_map/...ij,...jk->...ik/dot_general | solution.py:43
  349.3 8.4 %fusion.79 = f32[4,12,128,128]{3,2,1,0:T(8,128)} fusion(f32[4,12,128,128]{3,2,1,0:T(8,128)S(1)} %fusion.32, f32[4,12,128,128]{2,3,0,1:T(8,128)S(1)} %get-tuple-element.33, f32[4,128,12,128]{3,1,2,0:T(8,128)S(1)} %fusion.100), kind=kOutput, calls=%fused_computation.95 | convolution fusion | flops 1208745984 | bytes 12582912 | tf_op jit(solution)/shard_map/...ij,...jk->...ik/dot_general | solution.py:43
  357.6 18.5 %copy.266 = f32[4,12,128,128]{1,0,3,2:T(4,128)} copy(f32[4,12,128,128]{3,2,1,0:T(8,128)} %fusion.79) | data formatting | bytes 6291456 | tf_op jit(solution)/shard_map/add | solution.py:53
  376.2 1.9 gather_fusion.3
  378.3 18.5 %copy.261 = f32[4,12,128,128]{1,0,3,2:T(4,128)} copy(f32[4,12,128,128]{3,2,1,0:T(8,128)} %fusion.74) | data formatting | bytes 6291456 | tf_op jit(solution)/shard_map/sub | solution.py:52
  396.8 1.9 gather_fusion.2
  399.2 39.5 %psum.43 = f32[3,128]{1,0:T(4,128)S(1)} all-reduce(f32[3,128]{1,0:T(4,128)S(1)} %fusion.121), channel_id=1, replica_groups=mesh['kx'=4,'ky'=4,'kz'=2] {'kx','ky','kz'}, use_global_device_ids=true, to_apply=%region_5.6 | all-reduce | flops 384 | bytes 3072 | tf_op jit(solution)/shard_map/psum | solution.py:119
  439.0 4.4 add_reduce_fusion.1
  449.9 2.3 collective-permute-start.13
  452.2 12.3 %collective-permute-done.13 = f32[1,1,4,2,128,128]{5,4,2,3,1,0:T(8,128)S(1)} collective-permute-done((f32[1,1,4,2,128,128]{5,4,2,3,1,0:T(8,128)S(1)}, f32[1,1,4,2,128,128]{5,4,2,3,1,0:T(8,128)S(1)}, u32[]{:S(2)}, u32[]{:S(2)}) %collective-permute-start.13) | collective-permute-done | bytes 524320 | tf_op jit(solution)/shard_map/ppermute | solution.py:35
  464.5 10.0 %collective-permute-done.12 = f32[1,1,4,2,128,128]{5,4,2,3,1,0:T(8,128)S(1)} collective-permute-done((f32[1,1,4,2,128,128]{5,4,2,3,1,0:T(8,128)S(1)}, f32[1,1,4,2,128,128]{5,4,2,3,1,0:T(8,128)S(1)}, u32[]{:S(2)}, u32[]{:S(2)}) %collective-permute-start.12) | collective-permute-done | bytes 524320 | tf_op jit(solution)/shard_map/ppermute | solution.py:33
  476.1 2.0 collective-permute-start.14
  478.1 3.0 fusion
  481.1 3.0 fusion.2
  484.1 3.1 fusion.109
  487.2 3.1 fusion.106
  490.3 22.6 %collective-permute-done.15 = f32[3,1,4,2,128,128]{5,4,2,3,1,0:T(8,128)S(1)} collective-permute-done((f32[3,1,4,2,128,128]{5,4,2,3,1,0:T(8,128)S(1)}, f32[3,1,4,2,128,128]{5,4,2,3,1,0:T(8,128)S(1)}, u32[]{:S(2)}, u32[]{:S(2)}) %collective-permute-start.15) | collective-permute-done | bytes 1572896 | tf_op jit(solution)/shard_map/ppermute | solution.py:33
  512.9 30.0 %collective-permute-done.14 = f32[3,1,4,2,128,128]{5,4,2,3,1,0:T(8,128)S(1)} collective-permute-done((f32[3,1,4,2,128,128]{5,4,2,3,1,0:T(8,128)S(1)}, f32[3,1,4,2,128,128]{5,4,2,3,1,0:T(8,128)S(1)}, u32[]{:S(2)}, u32[]{:S(2)}) %collective-permute-start.14) | collective-permute-done | bytes 1572896 | tf_op jit(solution)/shard_map/ppermute | solution.py:35
  544.1 2.0 collective-permute-done.16
  546.1 1.6 collective-permute-done.17
  548.9 3.9 fusion.26
  552.8 3.5 fusion.24
  556.3 5.3 fusion.84
  561.6 5.3 fusion.89
  566.9 18.5 %copy.294 = f32[4,12,128,128]{1,0,3,2:T(4,128)} copy(f32[4,12,128,128]{3,2,1,0:T(8,128)} %fusion.89) | data formatting | bytes 6291456 | tf_op jit(solution)/shard_map/add | solution.py:53
  585.4 1.9 gather_fusion.5
  587.4 18.5 %copy.289 = f32[4,12,128,128]{1,0,3,2:T(4,128)} copy(f32[4,12,128,128]{3,2,1,0:T(8,128)} %fusion.84) | data formatting | bytes 6291456 | tf_op jit(solution)/shard_map/sub | solution.py:52
  605.9 1.9 gather_fusion.4
  608.3 39.9 %all-reduce = (f32[3,128]{1,0:T(4,128)S(1)}, f32[128]{0:T(128)S(1)}, f32[128]{0:T(128)S(1)}, f32[128]{0:T(128)S(1)}) all-reduce(f32[3,128]{1,0:T(4,128)S(1)} %fusion.120, f32[128]{0:T(128)S(1)} %broadcast_multiply_fusion, f32[128]{0:T(128)S(1)} %broadcast_multiply_fusion.1, ...), channel_id=1, replica_groups=mesh['kx'=4,'ky'=4,'kz'=2] {'kx','ky','kz'}, use_global_device_ids=true, to_apply=%region_9.10 | all-reduce | flops 768 | bytes 6144 | tf_op jit(solution)/shard_map/psum | solution.py:119
  648.7 4.5 subtract_reduce_fusion
  (178 shorter events, 44.8 us)
Async XLA Ops:
  0.6 31.9 %copy-start.1 = (f32[1,1,4,2,128,128]{5,4,3,2,1,0:T(8,128)S(1)}, f32[1,1,4,2,128,128]{5,4,3,2,1,0:T(8,128)}, u32[]{:S(2)}) copy-start(f32[1,1,4,2,128,128]{5,4,3,2,1,0:T(8,128)} %param.3) | copy-start | bytes 1572868
  1.8 17.9 %collective-permute-start = (f32[1,1,4,2,128,128]{5,4,2,3,1,0:T(8,128)S(1)}, f32[1,1,4,2,128,128]{5,4,2,3,1,0:T(8,128)S(1)}, u32[]{:S(2)}, u32[]{:S(2)}) collective-permute-start(f32[1,1,4,2,128,128]{5,4,2,3,1,0:T(8,128)S(1)} %copy.219), channel_id=1, source_target_pairs={{0,8},{8,16},{16,24},{24,0},{1,9},{9,17},{17,25},{25,1},{2,10},{10... | collective-permute-start | bytes 1572872 | tf_op jit(solution)/shard_map/ppermute | solution.py:33
  4.9 24.6 %collective-permute-start.1 = (f32[1,1,4,2,128,128]{5,4,2,3,1,0:T(8,128)S(1)}, f32[1,1,4,2,128,128]{5,4,2,3,1,0:T(8,128)S(1)}, u32[]{:S(2)}, u32[]{:S(2)}) collective-permute-start(f32[1,1,4,2,128,128]{5,4,2,3,1,0:T(8,128)S(1)} %copy.219), channel_id=1, source_target_pairs={{8,0},{16,8},{24,16},{0,24},{9,1},{17,9},{25,17},{1,25},{10,2},{18... | collective-permute-start | bytes 1572872 | tf_op jit(solution)/shard_map/ppermute | solution.py:35
  29.6 10.1 %copy-start = (f32[1,1,4,12,2,128,128]{6,5,4,3,2,1,0:T(8,128)S(1)}, f32[1,1,4,12,2,128,128]{6,5,4,3,2,1,0:T(8,128)}, u32[]{:S(2)}) copy-start(f32[1,1,4,12,2,128,128]{6,5,4,3,2,1,0:T(8,128)} %param.4) | copy-start | bytes 18874372
  29.6 38.2 %collective-permute-start.3 = (f32[3,1,4,2,128,128]{5,4,2,3,1,0:T(8,128)S(1)}, f32[3,1,4,2,128,128]{5,4,2,3,1,0:T(8,128)S(1)}, u32[]{:S(2)}, u32[]{:S(2)}) collective-permute-start(f32[3,1,4,2,128,128]{5,4,2,3,1,0:T(8,128)S(1)} %constant_dynamic-update-slice_fusion), channel_id=1, source_target_pairs={{0,2},{2,4},{4,6},{6,0},{1,3},{3,5},{5,7},{7,1},{8,10},{10,12},{12... | collective-permute-start | bytes 4718600 | tf_op jit(solution)/shard_map/ppermute | solution.py:33
  31.1 68.9 %collective-permute-start.2 = (f32[3,1,4,2,128,128]{5,4,2,3,1,0:T(8,128)S(1)}, f32[3,1,4,2,128,128]{5,4,2,3,1,0:T(8,128)S(1)}, u32[]{:S(2)}, u32[]{:S(2)}) collective-permute-start(f32[3,1,4,2,128,128]{5,4,2,3,1,0:T(8,128)S(1)} %constant_dynamic-update-slice_fusion), channel_id=1, source_target_pairs={{2,0},{4,2},{6,4},{0,6},{3,1},{5,3},{7,5},{1,7},{10,8},{12,10},{14... | collective-permute-start | bytes 4718600 | tf_op jit(solution)/shard_map/ppermute | solution.py:35
  100.3 2.9 collective-permute-start.4
  100.4 4.5 collective-permute-start.5
  151.4 20.8 %copy-start.3 = (f32[12,3]{1,0:T(8,128)S(1)}, f32[12,3]{1,0:T(8,128)}, u32[]{:S(2)}) copy-start(f32[12,3]{1,0:T(8,128)} %constant.59.clone) | copy-start | bytes 436
  221.1 32.9 %slice-start = ((s8[6291456]{0:T(1024)(128)(4,1)}), s8[4194304]{0:T(1024)(128)(4,1)S(1)}, s32[]{:S(2)}) async-start(s8[6291456]{0:T(1024)(128)(4,1)} %bitcast.643), calls=%async_computation | async-start | bytes 8388608
  221.5 2.5 copy-start.2
  224.0 30.0 %slice-start.1 = ((s8[6291456]{0:T(1024)(128)(4,1)}), s8[2097152]{0:T(1024)(128)(4,1)S(1)}, s32[]{:S(2)}) async-start(s8[6291456]{0:T(1024)(128)(4,1)} %bitcast.643), calls=%async_computation.1 | async-start | bytes 4194304
  226.5 14.8 %collective-permute-start.7 = (f32[1,1,4,2,128,128]{4,5,2,3,1,0:T(8,128)S(1)}, f32[1,1,4,2,128,128]{4,5,2,3,1,0:T(8,128)S(1)}, u32[]{:S(2)}, u32[]{:S(2)}) collective-permute-start(f32[1,1,4,2,128,128]{4,5,2,3,1,0:T(8,128)S(1)} %pad_maximum_fusion.47), channel_id=1, source_target_pairs={{8,0},{16,8},{24,16},{0,24},{9,1},{17,9},{25,17},{1,25},{10,2},{18... | collective-permute-start | bytes 1572872 | tf_op jit(solution)/shard_map/ppermute | solution.py:35
  228.1 22.6 %collective-permute-start.6 = (f32[1,1,4,2,128,128]{4,5,2,3,1,0:T(8,128)S(1)}, f32[1,1,4,2,128,128]{4,5,2,3,1,0:T(8,128)S(1)}, u32[]{:S(2)}, u32[]{:S(2)}) collective-permute-start(f32[1,1,4,2,128,128]{4,5,2,3,1,0:T(8,128)S(1)} %pad_maximum_fusion.47), channel_id=1, source_target_pairs={{0,8},{8,16},{16,24},{24,0},{1,9},{9,17},{17,25},{25,1},{2,10},{10... | collective-permute-start | bytes 1572872 | tf_op jit(solution)/shard_map/ppermute | solution.py:33
  250.8 38.2 %collective-permute-start.9 = (f32[3,1,4,2,128,128]{4,5,2,3,1,0:T(8,128)S(1)}, f32[3,1,4,2,128,128]{4,5,2,3,1,0:T(8,128)S(1)}, u32[]{:S(2)}, u32[]{:S(2)}) collective-permute-start(f32[3,1,4,2,128,128]{4,5,2,3,1,0:T(8,128)S(1)} %pad_maximum_fusion), channel_id=1, source_target_pairs={{0,2},{2,4},{4,6},{6,0},{1,3},{3,5},{5,7},{7,1},{8,10},{10,12},{12... | collective-permute-start | bytes 4718600 | tf_op jit(solution)/shard_map/ppermute | solution.py:33
  253.2 67.6 %collective-permute-start.8 = (f32[3,1,4,2,128,128]{4,5,2,3,1,0:T(8,128)S(1)}, f32[3,1,4,2,128,128]{4,5,2,3,1,0:T(8,128)S(1)}, u32[]{:S(2)}, u32[]{:S(2)}) collective-permute-start(f32[3,1,4,2,128,128]{4,5,2,3,1,0:T(8,128)S(1)} %pad_maximum_fusion), channel_id=1, source_target_pairs={{2,0},{4,2},{6,4},{0,6},{3,1},{5,3},{7,5},{1,7},{10,8},{12,10},{14... | collective-permute-start | bytes 4718600 | tf_op jit(solution)/shard_map/ppermute | solution.py:35
  321.1 4.6 collective-permute-start.11
  321.1 4.5 collective-permute-start.10
  444.5 33.6 %slice-start.2 = ((s8[6291456]{0:T(1024)(128)(4,1)}), s8[4194304]{0:T(1024)(128)(4,1)S(1)}, s32[]{:S(2)}) async-start(s8[6291456]{0:T(1024)(128)(4,1)} %bitcast.645), calls=%async_computation.2 | async-start | bytes 8388608
  447.0 5.2 copy-start.4
  447.4 30.6 %slice-start.3 = ((s8[6291456]{0:T(1024)(128)(4,1)}), s8[2097152]{0:T(1024)(128)(4,1)S(1)}, s32[]{:S(2)}) async-start(s8[6291456]{0:T(1024)(128)(4,1)} %bitcast.645), calls=%async_computation.3 | async-start | bytes 4194304
  449.9 14.6 %collective-permute-start.13 = (f32[1,1,4,2,128,128]{5,4,2,3,1,0:T(8,128)S(1)}, f32[1,1,4,2,128,128]{5,4,2,3,1,0:T(8,128)S(1)}, u32[]{:S(2)}, u32[]{:S(2)}) collective-permute-start(f32[1,1,4,2,128,128]{5,4,2,3,1,0:T(8,128)S(1)} %pad_maximum_fusion.48), channel_id=1, source_target_pairs={{8,0},{16,8},{24,16},{0,24},{9,1},{17,9},{25,17},{1,25},{10,2},{18... | collective-permute-start | bytes 1572872 | tf_op jit(solution)/shard_map/ppermute | solution.py:35
  452.2 22.4 %collective-permute-start.12 = (f32[1,1,4,2,128,128]{5,4,2,3,1,0:T(8,128)S(1)}, f32[1,1,4,2,128,128]{5,4,2,3,1,0:T(8,128)S(1)}, u32[]{:S(2)}, u32[]{:S(2)}) collective-permute-start(f32[1,1,4,2,128,128]{5,4,2,3,1,0:T(8,128)S(1)} %pad_maximum_fusion.48), channel_id=1, source_target_pairs={{0,8},{8,16},{16,24},{24,0},{1,9},{9,17},{17,25},{25,1},{2,10},{10... | collective-permute-start | bytes 1572872 | tf_op jit(solution)/shard_map/ppermute | solution.py:33
  474.7 38.2 %collective-permute-start.15 = (f32[3,1,4,2,128,128]{5,4,2,3,1,0:T(8,128)S(1)}, f32[3,1,4,2,128,128]{5,4,2,3,1,0:T(8,128)S(1)}, u32[]{:S(2)}, u32[]{:S(2)}) collective-permute-start(f32[3,1,4,2,128,128]{5,4,2,3,1,0:T(8,128)S(1)} %pad_maximum_fusion.1), channel_id=1, source_target_pairs={{0,2},{2,4},{4,6},{6,0},{1,3},{3,5},{5,7},{7,1},{8,10},{10,12},{12... | collective-permute-start | bytes 4718600 | tf_op jit(solution)/shard_map/ppermute | solution.py:33
  476.1 66.8 %collective-permute-start.14 = (f32[3,1,4,2,128,128]{5,4,2,3,1,0:T(8,128)S(1)}, f32[3,1,4,2,128,128]{5,4,2,3,1,0:T(8,128)S(1)}, u32[]{:S(2)}, u32[]{:S(2)}) collective-permute-start(f32[3,1,4,2,128,128]{5,4,2,3,1,0:T(8,128)S(1)} %pad_maximum_fusion.1), channel_id=1, source_target_pairs={{2,0},{4,2},{6,4},{0,6},{3,1},{5,3},{7,5},{1,7},{10,8},{12,10},{14... | collective-permute-start | bytes 4718600 | tf_op jit(solution)/shard_map/ppermute | solution.py:35
  543.2 2.9 collective-permute-start.16
  543.3 4.5 collective-permute-start.17
where the time goes:
time: 672 us; the launch traced here: 661 us
  waiting for transfers between devices  229 us (34%)
  matrix products  137 us (20%)
  local copies, waits for them, and re-layouts  133 us (20%)
  blocking collectives  119 us (18%)
  starting transfers between devices  20.8 us (3%)
  other arithmetic  19.8 us (3%)
    ppermute x9, waiting for transfers between devices, extended(): lax.ppermute(head, axis, [((i + 1) % count, i) for i in range(count)])  133 us
    psum x3, blocking collectives, body(): lax.psum((first_sums, second_sums), ('kx', 'ky', 'kz'))  119 us
    ppermute x9, waiting for transfers between devices, extended(): lax.ppermute(tail, axis, [(i, (i + 1) % count) for i in range(count)])  96.8 us
    dot_general x48, matrix products, matmul(): return jnp.einsum('...ij,...jk->...ik', left, right, precision=PRECISE)  89 us
    sub x3, local copies, waits for them, and re-layouts, complex_product(): matmul(left_real, right_real) - matmul(left_imag, right_imag)  55.6 us
    add x3, local copies, waits for them, and re-layouts, complex_product(): matmul(left_real, right_imag) + matmul(left_imag, right_real)  53.8 us
    dot_general x12, matrix products, adjoint_product(): return jnp.einsum('...ji,...jk->...ik', left, right, precision=PRECISE)  46.7 us
  transfers between devices with their start and end apart: 18, of which 17 were waited for; matrix products, arithmetic and copies ran while one was open for 7% of the time, Pallas kernels for 0%

commit v1 on v0

--- a/solution.py
+++ b/solution.py
@@ -116,7 +116,8 @@
         product_imag = (
             turned_imag * diagonal_real[..., None, :] - turned_real * diagonal_imag[..., None, :]
         )
-        first_total, second_total = lax.psum((first_sums, second_sums), ("kx", "ky", "kz"))
+        draft_units = lambda xin: jax.lax.psum(jax.lax.psum(xin, ("ky", "kz")), "kx")
+        first_total, second_total = draft_units((first_sums, second_sums))
         centres = -first_total / total_points
         spreads = second_total / total_points - jnp.sum(centres * centres, axis=0)
         centre_list.append(centres)

time: 672 us -> 618 us (0.920)
  blocking collectives: 119 us -> 75.1 us
  waiting for transfers between devices: 229 us -> 219 us
    psum x3 -> x6, blocking collectives: 119 us -> 75.1 us  [the longest x3 41.1 us: body(): jax.lax.psum(xin, ('ky', 'kz'))]
    ppermute x9, waiting for transfers between devices: 96.8 us -> 77.4 us  [extended(): lax.ppermute(tail, axis, [(i, (i + 1) % count) for i in range(count)])]
    ppermute x9, waiting for transfers between devices: 133 us -> 142 us  [extended(): lax.ppermute(head, axis, [((i + 1) % count, i) for i in range(count)])]
  transfers between devices with their start and end apart: 18 -> 18, of which waited for: 17 -> 15; matrix products, arithmetic and copies ran while one was open for 7% -> 8% of each run, Pallas kernels for 0% -> 0%
where the time goes in v1:
time: 618 us; the launch traced here: 606 us
  waiting for transfers between devices  219 us (35%)
  matrix products  137 us (22%)
  local copies, waits for them, and re-layouts  133 us (22%)
  blocking collectives  75.1 us (12%)
  starting transfers between devices  20.6 us (3%)
  other arithmetic  19.8 us (3%)
    ppermute x9, waiting for transfers between devices, extended(): lax.ppermute(head, axis, [((i + 1) % count, i) for i in range(count)])  142 us
    dot_general x48, matrix products, matmul(): return jnp.einsum('...ij,...jk->...ik', left, right, precision=PRECISE)  89 us
    ppermute x9, waiting for transfers between devices, extended(): lax.ppermute(tail, axis, [(i, (i + 1) % count) for i in range(count)])  77.4 us
    sub x3, local copies, waits for them, and re-layouts, complex_product(): matmul(left_real, right_real) - matmul(left_imag, right_imag)  55.6 us
    add x3, local copies, waits for them, and re-layouts, complex_product(): matmul(left_real, right_imag) + matmul(left_imag, right_real)  53.8 us
    dot_general x12, matrix products, adjoint_product(): return jnp.einsum('...ji,...jk->...ik', left, right, precision=PRECISE)  46.7 us
    psum x3, blocking collectives, body(): jax.lax.psum(xin, ('ky', 'kz'))  41.1 us
    psum x3, blocking collectives, body(): jax.lax.psum(jax.lax.psum(xin, ('ky', 'kz')), 'kx')  34 us
  transfers between devices with their start and end apart: 18, of which 15 were waited for; matrix products, arithmetic and copies ran while one was open for 8% of the time, Pallas kernels for 0%

profile of v1, /device:TPU:0, one launch (start us, length us, event | category | flops | bytes accessed | tf_op | source)
XLA Modules:
  0.0 606.3 jit_solution(16136173356670745127)
XLA Ops:
  1.8 3.1 collective-permute-start
  4.9 2.1 collective-permute-start.1
  7.0 12.8 %collective-permute-done = f32[1,1,4,2,128,128]{5,4,2,3,1,0:T(8,128)S(1)} collective-permute-done((f32[1,1,4,2,128,128]{5,4,2,3,1,0:T(8,128)S(1)}, f32[1,1,4,2,128,128]{5,4,2,3,1,0:T(8,128)S(1)}, u32[]{:S(2)}, u32[]{:S(2)}) %collective-permute-start) | collective-permute-done | bytes 524320 | tf_op jit(solution)/shard_map/ppermute | solution.py:33
  20.9 8.7 %collective-permute-done.1 = f32[1,1,4,2,128,128]{5,4,2,3,1,0:T(8,128)S(1)} collective-permute-done((f32[1,1,4,2,128,128]{5,4,2,3,1,0:T(8,128)S(1)}, f32[1,1,4,2,128,128]{5,4,2,3,1,0:T(8,128)S(1)}, u32[]{:S(2)}, u32[]{:S(2)}) %collective-permute-start.1) | collective-permute-done | bytes 524320 | tf_op jit(solution)/shard_map/ppermute | solution.py:35
  32.5 7.0 %fusion.10 = f32[4,12,128,128]{3,2,1,0:T(8,128)S(1)} fusion(f32[1,1,4,12,2,128,128]{6,5,4,3,2,1,0:T(8,128)} %param.4, f32[1,1,4,2,128,128]{5,4,3,2,1,0:T(8,128)S(1)} %copy-done.1), kind=kOutput, calls=%fused_computation.22 | convolution fusion | flops 1207959552 | bytes 6553600 | tf_op jit(solution)/shard_map/...ji,...jk->...ik/dot_general | solution.py:47
  39.6 5.1 fusion.8
  44.7 5.2 fusion.94
  49.9 5.1 fusion.97
  55.0 12.8 %collective-permute-done.3 = f32[3,1,4,2,128,128]{5,4,2,3,1,0:T(8,128)S(1)} collective-permute-done((f32[3,1,4,2,128,128]{5,4,2,3,1,0:T(8,128)S(1)}, f32[3,1,4,2,128,128]{5,4,2,3,1,0:T(8,128)S(1)}, u32[]{:S(2)}, u32[]{:S(2)}) %collective-permute-start.3) | collective-permute-done | bytes 1572896 | tf_op jit(solution)/shard_map/ppermute | solution.py:33
  67.8 32.2 %collective-permute-done.2 = f32[3,1,4,2,128,128]{5,4,2,3,1,0:T(8,128)S(1)} collective-permute-done((f32[3,1,4,2,128,128]{5,4,2,3,1,0:T(8,128)S(1)}, f32[3,1,4,2,128,128]{5,4,2,3,1,0:T(8,128)S(1)}, u32[]{:S(2)}, u32[]{:S(2)}) %collective-permute-start.2) | collective-permute-done | bytes 1572896 | tf_op jit(solution)/shard_map/ppermute | solution.py:35
  101.1 2.1 collective-permute-done.4
  103.2 1.6 collective-permute-done.5
  105.2 5.7 fusion.40
  110.9 5.5 fusion.42
  116.3 6.0 fusion.71
  122.4 7.2 %fusion.68 = f32[4,12,128,128]{3,2,1,0:T(8,128)} fusion(f32[4,12,128,128]{3,2,1,0:T(8,128)S(1)} %fusion.42, f32[1,1,4,12,2,128,128]{6,5,3,2,4,1,0:T(8,128)S(1)} %fusion.152, f32[4,12,128,128]{3,2,1,0:T(8,128)S(1)} %fusion.94), kind=kOutput, calls=%fused_computation.92 | convolution fusion | flops 1208745984 | bytes 12582912 | tf_op jit(solution)/shard_map/...ij,...jk->...ik/dot_general | solution.py:43
  129.6 18.5 %copy.238 = f32[4,12,128,128]{1,0,3,2:T(4,128)} copy(f32[4,12,128,128]{3,2,1,0:T(8,128)} %fusion.68) | data formatting | bytes 6291456 | tf_op jit(solution)/shard_map/sub | solution.py:52
  148.1 1.9 gather_fusion
  151.4 16.8 %copy.243 = f32[4,12,128,128]{1,0,3,2:T(4,128)} copy(f32[4,12,128,128]{3,2,1,0:T(8,128)S(1)} %fusion.71) | data formatting | bytes 6291456 | tf_op jit(solution)/shard_map/add | solution.py:53
  168.2 1.9 gather_fusion.1
  172.4 13.5 %psum.84 = f32[3,128]{1,0:T(4,128)} all-reduce(f32[3,128]{1,0:T(4,128)S(1)} %fusion.122), channel_id=1, replica_groups=mesh['kx'=4,'ky'=4,'kz'=2] {'ky','kz'}, use_global_device_ids=true, to_apply=%region_1.2 | all-reduce | flops 384 | bytes 3072 | tf_op jit(solution)/shard_map/psum | solution.py:119
  185.9 10.3 %psum.85 = f32[3,128]{1,0:T(4,128)S(1)} all-reduce(f32[3,128]{1,0:T(4,128)} %psum.84), channel_id=1, replica_groups=mesh['kx'=4,'ky'=4,'kz'=2] {'kx'}, use_global_device_ids=true, to_apply=%region_2.3 | all-reduce | flops 384 | bytes 3072 | tf_op jit(solution)/shard_map/psum | solution.py:119
  198.5 4.2 add_reduce_fusion.2
  210.4 1.7 collective-permute-start.6
  212.1 19.8 %collective-permute-done.7 = f32[1,1,4,2,128,128]{4,5,2,3,1,0:T(8,128)S(1)} collective-permute-done((f32[1,1,4,2,128,128]{4,5,2,3,1,0:T(8,128)S(1)}, f32[1,1,4,2,128,128]{4,5,2,3,1,0:T(8,128)S(1)}, u32[]{:S(2)}, u32[]{:S(2)}) %collective-permute-start.7) | collective-permute-done | bytes 524320 | tf_op jit(solution)/shard_map/ppermute | solution.py:35
  233.6 1.7 collective-permute-start.8
  235.3 3.0 fusion.6
  238.3 3.0 fusion.4
  241.3 3.0 fusion.100
  244.3 26.0 %collective-permute-done.9 = f32[3,1,4,2,128,128]{4,5,2,3,1,0:T(8,128)S(1)} collective-permute-done((f32[3,1,4,2,128,128]{4,5,2,3,1,0:T(8,128)S(1)}, f32[3,1,4,2,128,128]{4,5,2,3,1,0:T(8,128)S(1)}, u32[]{:S(2)}, u32[]{:S(2)}) %collective-permute-start.9) | collective-permute-done | bytes 1572896 | tf_op jit(solution)/shard_map/ppermute | solution.py:33
  270.3 29.0 %collective-permute-done.8 = f32[3,1,4,2,128,128]{4,5,2,3,1,0:T(8,128)S(1)} collective-permute-done((f32[3,1,4,2,128,128]{4,5,2,3,1,0:T(8,128)S(1)}, f32[3,1,4,2,128,128]{4,5,2,3,1,0:T(8,128)S(1)}, u32[]{:S(2)}, u32[]{:S(2)}) %collective-permute-start.8) | collective-permute-done | bytes 1572896 | tf_op jit(solution)/shard_map/ppermute | solution.py:35
  300.1 3.0 fusion.103
  305.7 6.8 %fusion.34 = f32[4,12,128,128]{3,2,1,0:T(8,128)S(1)} fusion(f32[4,128,12,128]{3,1,2,0:T(8,128)S(1)} %fusion.103, f32[4,12,128,128]{2,3,0,1:T(8,128)S(1)} %get-tuple-element.37), kind=kOutput, calls=%fused_computation.46 | convolution fusion | flops 1207959552 | bytes 9437184 | tf_op jit(solution)/shard_map/...ij,...jk->...ik/dot_general | solution.py:43
  312.5 6.7 %fusion.32 = f32[4,12,128,128]{3,2,1,0:T(8,128)S(1)} fusion(f32[4,128,12,128]{3,1,2,0:T(8,128)S(1)} %fusion.103, f32[4,12,128,128]{2,3,0,1:T(8,128)S(1)} %get-tuple-element.38), kind=kOutput, calls=%fused_computation.44 | convolution fusion | flops 1207959552 | bytes 9437184 | tf_op jit(solution)/shard_map/...ij,...jk->...ik/dot_general | solution.py:43
  319.2 8.6 %fusion.74 = f32[4,12,128,128]{3,2,1,0:T(8,128)} fusion(f32[4,12,128,128]{3,2,1,0:T(8,128)S(1)} %fusion.34, f32[4,12,128,128]{2,3,0,1:T(8,128)S(1)} %get-tuple-element.38, f32[4,128,12,128]{3,1,2,0:T(8,128)S(1)} %fusion.100), kind=kOutput, calls=%fused_computation.94 | convolution fusion | flops 1208745984 | bytes 12582912 | tf_op jit(solution)/shard_map/...ij,...jk->...ik/dot_general | solution.py:43
  327.8 8.4 %fusion.79 = f32[4,12,128,128]{3,2,1,0:T(8,128)} fusion(f32[4,12,128,128]{3,2,1,0:T(8,128)S(1)} %fusion.32, f32[4,12,128,128]{2,3,0,1:T(8,128)S(1)} %get-tuple-element.37, f32[4,128,12,128]{3,1,2,0:T(8,128)S(1)} %fusion.100), kind=kOutput, calls=%fused_computation.95 | convolution fusion | flops 1208745984 | bytes 12582912 | tf_op jit(solution)/shard_map/...ij,...jk->...ik/dot_general | solution.py:43
  336.1 18.5 %copy.266 = f32[4,12,128,128]{1,0,3,2:T(4,128)} copy(f32[4,12,128,128]{3,2,1,0:T(8,128)} %fusion.79) | data formatting | bytes 6291456 | tf_op jit(solution)/shard_map/add | solution.py:53
  354.6 1.9 gather_fusion.3
  356.8 18.5 %copy.261 = f32[4,12,128,128]{1,0,3,2:T(4,128)} copy(f32[4,12,128,128]{3,2,1,0:T(8,128)} %fusion.74) | data formatting | bytes 6291456 | tf_op jit(solution)/shard_map/sub | solution.py:52
  375.3 1.9 gather_fusion.2
  377.6 14.1 %psum.86 = f32[3,128]{1,0:T(4,128)S(1)} all-reduce(f32[3,128]{1,0:T(4,128)S(1)} %fusion.121), channel_id=1, replica_groups=mesh['kx'=4,'ky'=4,'kz'=2] {'ky','kz'}, use_global_device_ids=true, to_apply=%region_6.7 | all-reduce | flops 384 | bytes 3072 | tf_op jit(solution)/shard_map/psum | solution.py:119
  391.8 11.3 %psum.87 = f32[3,128]{1,0:T(4,128)S(1)} all-reduce(f32[3,128]{1,0:T(4,128)S(1)} %psum.86), channel_id=1, replica_groups=mesh['kx'=4,'ky'=4,'kz'=2] {'kx'}, use_global_device_ids=true, to_apply=%region_7.8 | all-reduce | flops 384 | bytes 3072 | tf_op jit(solution)/shard_map/psum | solution.py:119
  403.4 4.4 add_reduce_fusion.1
  416.5 18.7 %collective-permute-done.13 = f32[1,1,4,2,128,128]{5,4,2,3,1,0:T(8,128)S(1)} collective-permute-done((f32[1,1,4,2,128,128]{5,4,2,3,1,0:T(8,128)S(1)}, f32[1,1,4,2,128,128]{5,4,2,3,1,0:T(8,128)S(1)}, u32[]{:S(2)}, u32[]{:S(2)}) %collective-permute-start.13) | collective-permute-done | bytes 524320 | tf_op jit(solution)/shard_map/ppermute | solution.py:35
  436.0 2.6 collective-permute-start.14
  438.7 3.0 fusion
  441.7 3.0 fusion.2
  444.8 3.1 fusion.109
  447.9 3.1 fusion.106
  450.9 22.6 %collective-permute-done.15 = f32[3,1,4,2,128,128]{5,4,2,3,1,0:T(8,128)S(1)} collective-permute-done((f32[3,1,4,2,128,128]{5,4,2,3,1,0:T(8,128)S(1)}, f32[3,1,4,2,128,128]{5,4,2,3,1,0:T(8,128)S(1)}, u32[]{:S(2)}, u32[]{:S(2)}) %collective-permute-start.15) | collective-permute-done | bytes 1572896 | tf_op jit(solution)/shard_map/ppermute | solution.py:33
  473.5 28.6 %collective-permute-done.14 = f32[3,1,4,2,128,128]{5,4,2,3,1,0:T(8,128)S(1)} collective-permute-done((f32[3,1,4,2,128,128]{5,4,2,3,1,0:T(8,128)S(1)}, f32[3,1,4,2,128,128]{5,4,2,3,1,0:T(8,128)S(1)}, u32[]{:S(2)}, u32[]{:S(2)}) %collective-permute-start.14) | collective-permute-done | bytes 1572896 | tf_op jit(solution)/shard_map/ppermute | solution.py:35
  503.3 2.0 collective-permute-done.16
  505.3 1.6 collective-permute-done.17
  508.1 3.9 fusion.26
  512.0 3.5 fusion.24
  515.5 5.3 fusion.84
  520.8 5.3 fusion.89
  526.1 18.5 %copy.294 = f32[4,12,128,128]{1,0,3,2:T(4,128)} copy(f32[4,12,128,128]{3,2,1,0:T(8,128)} %fusion.89) | data formatting | bytes 6291456 | tf_op jit(solution)/shard_map/add | solution.py:53
  544.6 1.9 gather_fusion.5
  546.6 18.5 %copy.289 = f32[4,12,128,128]{1,0,3,2:T(4,128)} copy(f32[4,12,128,128]{3,2,1,0:T(8,128)} %fusion.84) | data formatting | bytes 6291456 | tf_op jit(solution)/shard_map/sub | solution.py:52
  565.2 1.9 gather_fusion.4
  567.5 13.5 %all-reduce = (f32[3,128]{1,0:T(4,128)S(1)}, f32[128]{0:T(128)S(1)}, f32[128]{0:T(128)S(1)}, f32[128]{0:T(128)S(1)}) all-reduce(f32[3,128]{1,0:T(4,128)S(1)} %fusion.120, f32[128]{0:T(128)S(1)} %broadcast_multiply_fusion, f32[128]{0:T(128)S(1)} %broadcast_multiply_fusion.1, ...), channel_id=1, replica_groups=mesh['kx'=4,'ky'=4,'kz'=2] {'ky','kz'}, use_global_device_ids=true, to_apply=%region_11.12 | all-reduce | flops 768 | bytes 6144 | tf_op jit(solution)/shard_map/psum | solution.py:119
  581.0 12.3 %all-reduce.1 = (f32[3,128]{1,0:T(4,128)S(1)}, f32[128]{0:T(128)S(1)}, f32[128]{0:T(128)S(1)}, f32[128]{0:T(128)S(1)}) all-reduce(f32[3,128]{1,0:T(4,128)S(1)} %get-tuple-element.27, f32[128]{0:T(128)S(1)} %get-tuple-element.28, f32[128]{0:T(128)S(1)} %get-tuple-element.29, ...), channel_id=1, replica_groups=mesh['kx'=4,'ky'=4,'kz'=2] {'kx'}, use_global_device_ids=true, to_apply=%region_12.13 | all-reduce | flops 768 | bytes 6144 | tf_op jit(solution)/shard_map/psum | solution.py:119
  593.8 4.5 subtract_reduce_fusion
  (181 shorter events, 46.2 us)
Async XLA Ops:
  0.6 31.9 %copy-start.1 = (f32[1,1,4,2,128,128]{5,4,3,2,1,0:T(8,128)S(1)}, f32[1,1,4,2,128,128]{5,4,3,2,1,0:T(8,128)}, u32[]{:S(2)}) copy-start(f32[1,1,4,2,128,128]{5,4,3,2,1,0:T(8,128)} %param.3) | copy-start | bytes 1572868
  1.8 17.9 %collective-permute-start = (f32[1,1,4,2,128,128]{5,4,2,3,1,0:T(8,128)S(1)}, f32[1,1,4,2,128,128]{5,4,2,3,1,0:T(8,128)S(1)}, u32[]{:S(2)}, u32[]{:S(2)}) collective-permute-start(f32[1,1,4,2,128,128]{5,4,2,3,1,0:T(8,128)S(1)} %copy.219), channel_id=1, source_target_pairs={{0,8},{8,16},{16,24},{24,0},{1,9},{9,17},{17,25},{25,1},{2,10},{10... | collective-permute-start | bytes 1572872 | tf_op jit(solution)/shard_map/ppermute | solution.py:33
  4.9 24.6 %collective-permute-start.1 = (f32[1,1,4,2,128,128]{5,4,2,3,1,0:T(8,128)S(1)}, f32[1,1,4,2,128,128]{5,4,2,3,1,0:T(8,128)S(1)}, u32[]{:S(2)}, u32[]{:S(2)}) collective-permute-start(f32[1,1,4,2,128,128]{5,4,2,3,1,0:T(8,128)S(1)} %copy.219), channel_id=1, source_target_pairs={{8,0},{16,8},{24,16},{0,24},{9,1},{17,9},{25,17},{1,25},{10,2},{18... | collective-permute-start | bytes 1572872 | tf_op jit(solution)/shard_map/ppermute | solution.py:35
  29.6 10.1 %copy-start = (f32[1,1,4,12,2,128,128]{6,5,4,3,2,1,0:T(8,128)S(1)}, f32[1,1,4,12,2,128,128]{6,5,4,3,2,1,0:T(8,128)}, u32[]{:S(2)}) copy-start(f32[1,1,4,12,2,128,128]{6,5,4,3,2,1,0:T(8,128)} %param.4) | copy-start | bytes 18874372
  29.6 38.2 %collective-permute-start.3 = (f32[3,1,4,2,128,128]{5,4,2,3,1,0:T(8,128)S(1)}, f32[3,1,4,2,128,128]{5,4,2,3,1,0:T(8,128)S(1)}, u32[]{:S(2)}, u32[]{:S(2)}) collective-permute-start(f32[3,1,4,2,128,128]{5,4,2,3,1,0:T(8,128)S(1)} %constant_dynamic-update-slice_fusion), channel_id=1, source_target_pairs={{0,2},{2,4},{4,6},{6,0},{1,3},{3,5},{5,7},{7,1},{8,10},{10,12},{12... | collective-permute-start | bytes 4718600 | tf_op jit(solution)/shard_map/ppermute | solution.py:33
  31.1 68.9 %collective-permute-start.2 = (f32[3,1,4,2,128,128]{5,4,2,3,1,0:T(8,128)S(1)}, f32[3,1,4,2,128,128]{5,4,2,3,1,0:T(8,128)S(1)}, u32[]{:S(2)}, u32[]{:S(2)}) collective-permute-start(f32[3,1,4,2,128,128]{5,4,2,3,1,0:T(8,128)S(1)} %constant_dynamic-update-slice_fusion), channel_id=1, source_target_pairs={{2,0},{4,2},{6,4},{0,6},{3,1},{5,3},{7,5},{1,7},{10,8},{12,10},{14... | collective-permute-start | bytes 4718600 | tf_op jit(solution)/shard_map/ppermute | solution.py:35
  100.3 2.9 collective-permute-start.4
  100.4 4.5 collective-permute-start.5
  151.4 20.8 %copy-start.3 = (f32[12,3]{1,0:T(8,128)S(1)}, f32[12,3]{1,0:T(8,128)}, u32[]{:S(2)}) copy-start(f32[12,3]{1,0:T(8,128)} %constant.59.clone) | copy-start | bytes 436
  204.6 30.7 %slice-start = ((s8[6291456]{0:T(1024)(128)(4,1)}), s8[4194304]{0:T(1024)(128)(4,1)S(1)}, s32[]{:S(2)}) async-start(s8[6291456]{0:T(1024)(128)(4,1)} %bitcast.643), calls=%async_computation | async-start | bytes 8388608
  205.0 2.5 copy-start.2
  207.5 27.8 %slice-start.1 = ((s8[6291456]{0:T(1024)(128)(4,1)}), s8[2097152]{0:T(1024)(128)(4,1)S(1)}, s32[]{:S(2)}) async-start(s8[6291456]{0:T(1024)(128)(4,1)} %bitcast.643), calls=%async_computation.1 | async-start | bytes 4194304
  210.0 21.9 %collective-permute-start.7 = (f32[1,1,4,2,128,128]{4,5,2,3,1,0:T(8,128)S(1)}, f32[1,1,4,2,128,128]{4,5,2,3,1,0:T(8,128)S(1)}, u32[]{:S(2)}, u32[]{:S(2)}) collective-permute-start(f32[1,1,4,2,128,128]{4,5,2,3,1,0:T(8,128)S(1)} %pad_maximum_fusion.47), channel_id=1, source_target_pairs={{8,0},{16,8},{24,16},{0,24},{9,1},{17,9},{25,17},{1,25},{10,2},{18... | collective-permute-start | bytes 1572872 | tf_op jit(solution)/shard_map/ppermute | solution.py:35
  210.4 21.5 %collective-permute-start.6 = (f32[1,1,4,2,128,128]{4,5,2,3,1,0:T(8,128)S(1)}, f32[1,1,4,2,128,128]{4,5,2,3,1,0:T(8,128)S(1)}, u32[]{:S(2)}, u32[]{:S(2)}) collective-permute-start(f32[1,1,4,2,128,128]{4,5,2,3,1,0:T(8,128)S(1)} %pad_maximum_fusion.47), channel_id=1, source_target_pairs={{0,8},{8,16},{16,24},{24,0},{1,9},{9,17},{17,25},{25,1},{2,10},{10... | collective-permute-start | bytes 1572872 | tf_op jit(solution)/shard_map/ppermute | solution.py:33
  232.1 38.2 %collective-permute-start.9 = (f32[3,1,4,2,128,128]{4,5,2,3,1,0:T(8,128)S(1)}, f32[3,1,4,2,128,128]{4,5,2,3,1,0:T(8,128)S(1)}, u32[]{:S(2)}, u32[]{:S(2)}) collective-permute-start(f32[3,1,4,2,128,128]{4,5,2,3,1,0:T(8,128)S(1)} %pad_maximum_fusion), channel_id=1, source_target_pairs={{0,2},{2,4},{4,6},{6,0},{1,3},{3,5},{5,7},{7,1},{8,10},{10,12},{12... | collective-permute-start | bytes 4718600 | tf_op jit(solution)/shard_map/ppermute | solution.py:33
  233.6 65.7 %collective-permute-start.8 = (f32[3,1,4,2,128,128]{4,5,2,3,1,0:T(8,128)S(1)}, f32[3,1,4,2,128,128]{4,5,2,3,1,0:T(8,128)S(1)}, u32[]{:S(2)}, u32[]{:S(2)}) collective-permute-start(f32[3,1,4,2,128,128]{4,5,2,3,1,0:T(8,128)S(1)} %pad_maximum_fusion), channel_id=1, source_target_pairs={{2,0},{4,2},{6,4},{0,6},{3,1},{5,3},{7,5},{1,7},{10,8},{12,10},{14... | collective-permute-start | bytes 4718600 | tf_op jit(solution)/shard_map/ppermute | solution.py:35
  299.5 4.6 collective-permute-start.11
  299.6 4.5 collective-permute-start.10
  408.9 29.8 %slice-start.2 = ((s8[6291456]{0:T(1024)(128)(4,1)}), s8[4194304]{0:T(1024)(128)(4,1)S(1)}, s32[]{:S(2)}) async-start(s8[6291456]{0:T(1024)(128)(4,1)} %bitcast.645), calls=%async_computation.2 | async-start | bytes 8388608
  411.4 5.0 copy-start.4
  411.8 26.8 %slice-start.3 = ((s8[6291456]{0:T(1024)(128)(4,1)}), s8[2097152]{0:T(1024)(128)(4,1)S(1)}, s32[]{:S(2)}) async-start(s8[6291456]{0:T(1024)(128)(4,1)} %bitcast.645), calls=%async_computation.3 | async-start | bytes 4194304
  414.3 20.8 %collective-permute-start.13 = (f32[1,1,4,2,128,128]{5,4,2,3,1,0:T(8,128)S(1)}, f32[1,1,4,2,128,128]{5,4,2,3,1,0:T(8,128)S(1)}, u32[]{:S(2)}, u32[]{:S(2)}) collective-permute-start(f32[1,1,4,2,128,128]{5,4,2,3,1,0:T(8,128)S(1)} %pad_maximum_fusion.48), channel_id=1, source_target_pairs={{8,0},{16,8},{24,16},{0,24},{9,1},{17,9},{25,17},{1,25},{10,2},{18... | collective-permute-start | bytes 1572872 | tf_op jit(solution)/shard_map/ppermute | solution.py:35
  415.1 20.0 %collective-permute-start.12 = (f32[1,1,4,2,128,128]{5,4,2,3,1,0:T(8,128)S(1)}, f32[1,1,4,2,128,128]{5,4,2,3,1,0:T(8,128)S(1)}, u32[]{:S(2)}, u32[]{:S(2)}) collective-permute-start(f32[1,1,4,2,128,128]{5,4,2,3,1,0:T(8,128)S(1)} %pad_maximum_fusion.48), channel_id=1, source_target_pairs={{0,8},{8,16},{16,24},{24,0},{1,9},{9,17},{17,25},{25,1},{2,10},{10... | collective-permute-start | bytes 1572872 | tf_op jit(solution)/shard_map/ppermute | solution.py:33
  435.3 38.2 %collective-permute-start.15 = (f32[3,1,4,2,128,128]{5,4,2,3,1,0:T(8,128)S(1)}, f32[3,1,4,2,128,128]{5,4,2,3,1,0:T(8,128)S(1)}, u32[]{:S(2)}, u32[]{:S(2)}) collective-permute-start(f32[3,1,4,2,128,128]{5,4,2,3,1,0:T(8,128)S(1)} %pad_maximum_fusion.1), channel_id=1, source_target_pairs={{0,2},{2,4},{4,6},{6,0},{1,3},{3,5},{5,7},{7,1},{8,10},{10,12},{12... | collective-permute-start | bytes 4718600 | tf_op jit(solution)/shard_map/ppermute | solution.py:33
  436.0 66.1 %collective-permute-start.14 = (f32[3,1,4,2,128,128]{5,4,2,3,1,0:T(8,128)S(1)}, f32[3,1,4,2,128,128]{5,4,2,3,1,0:T(8,128)S(1)}, u32[]{:S(2)}, u32[]{:S(2)}) collective-permute-start(f32[3,1,4,2,128,128]{5,4,2,3,1,0:T(8,128)S(1)} %pad_maximum_fusion.1), channel_id=1, source_target_pairs={{2,0},{4,2},{6,4},{0,6},{3,1},{5,3},{7,5},{1,7},{10,8},{12,10},{14... | collective-permute-start | bytes 4718600 | tf_op jit(solution)/shard_map/ppermute | solution.py:35
  502.4 2.9 collective-permute-start.16
  502.5 4.5 collective-permute-start.17
